TPU v7x, 32 devices: a whole 2x2x4 slice. The times are simulated.
32 devices in a mesh: copies: 2 (over y), oct: 4 (over z), leaf: 4 (over x, core).
Axes of the slice: x: 2, y: 2, z: 4, core: 2. Of those that a mesh axis runs over, the one named last changes fastest.
Arguments:
- coords: float32 [3, 65536], P(None, ('copies', 'oct')), parts along dimension 1, may hold values from 0 to 1, as said below
- skeleton: float32 [3, 32, 128], P(None, None, 'copies'), parts along dimension 2, may hold values from 0 to 1, as said below
- basis: bfloat16 [32, 65536], P(None, ('copies', 'oct', 'leaf')), parts along dimension 1, may hold values from -1.5 to 1.5
- probes: bfloat16 [65536, 128], P(('copies', 'oct', 'leaf')), parts along dimension 0, may hold values from -6 to 6
- near_list: int32 [128, 27], P(('copies', 'oct', 'leaf')), parts along dimension 0, may hold values from 0 to 63, as said below
- far_list: int32 [128, 32], P('copies'), parts along dimension 0, may hold values from 0 to 63, as said below
Outputs:
- product: bfloat16 [65536, 128], P(('copies', 'oct', 'leaf')), parts along dimension 0
There are 2 independent parts, one for each index of `copies`. A program takes and returns all parts, laid end to end along the dimension named above; each array names one. Nothing has to cross between parts.
Inputs may be any that keep to these rules, and one draw needn't show every extreme that they name: `coords`: the points of leaf block b lie in b's octree cell, whose corner follows from the bits of b taken in turn for the three components. The skeleton points of leaf block b lie in b's octree cell. `near_list`: entry 0 of row a is a. The other entries name leaf blocks of a's octant group held by a's device d = a // 4 or by the device just before or after it along leaf within the group; entries may repeat. `far_list`: every entry names a leaf block of another octant group than its row's (group = block // 16). Among the rows of one device, the entries that name blocks of any one other device number at most 11, and exactly 11 for some device; entries may repeat.
All inputs are finite; a program needn't handle non-finite values.
Results may differ from a plain program's by a relative error of at most 0.005.
Values may be sent and summed in bfloat16 or wider, within the bound.
A program may use at most 64 MiB of HBM per device.

v0:
```python
import math

import jax
import jax.numpy as jnp
from jax import lax
from jax.sharding import PartitionSpec as P

LEAF = 512
RANK = 32
RHS = 128
NEAR = 27
FAR = 32


length_scale = 0.4
root_three = math.sqrt(3.0)


def extended(block, sides, width):
    for axis, dim in sides:
        count = lax.axis_size(axis)
        forward = [(i, i + 1) for i in range(count - 1)]
        backward = [(target, source) for source, target in forward]
        low = lax.ppermute(
            lax.slice_in_dim(block, block.shape[dim] - width, None, axis=dim), axis, forward
        )
        high = lax.ppermute(lax.slice_in_dim(block, 0, width, axis=dim), axis, backward)
        block = jnp.concatenate([low, block, high], axis=dim)
    return block


def matern(dist_sq):
    scaled = jnp.sqrt(dist_sq) * (root_three / length_scale)
    return (1.0 + scaled) * jnp.exp(-scaled)


def outgoing_slots(coef, far_list, far_flat, per_dev, dev_pos, device_count, leaf_count):
    requests = per_dev * FAR
    others = device_count - leaf_count
    slots = (requests + others - 1) // others
    owner_all = (far_list // per_dev).reshape(device_count, requests)
    local_all = (far_list % per_dev).reshape(device_count, requests)
    mine_mask = jnp.where(owner_all == dev_pos, 1.0, 0.0).astype(jnp.bfloat16)
    strict = jnp.where(
        lax.broadcasted_iota(jnp.int32, (requests, requests), 0)
        < lax.broadcasted_iota(jnp.int32, (requests, requests), 1),
        1.0,
        0.0,
    ).astype(jnp.bfloat16)
    rank_mine = jnp.dot(mine_mask, strict, preferred_element_type=jnp.float32)
    slot_ids = jnp.arange(slots, dtype=jnp.float32)
    slot_hot = jnp.where(
        (owner_all[:, :, None] == dev_pos) & (rank_mine[:, :, None] == slot_ids[None, None, :]),
        1.0,
        0.0,
    ).astype(jnp.bfloat16)
    leaf_hot = jnp.where(
        local_all[:, :, None] == jnp.arange(per_dev, dtype=jnp.int32)[None, None, :], 1.0, 0.0
    ).astype(jnp.bfloat16)
    selector = jnp.einsum(
        "rqs,rqj->rsj", slot_hot, leaf_hot, preferred_element_type=jnp.float32
    ).astype(jnp.bfloat16)
    outgoing = jnp.einsum(
        "rsj,jmh->rsmh", selector, coef, preferred_element_type=jnp.float32
    ).astype(jnp.bfloat16)
    own_owner = far_flat // per_dev
    same_owner = own_owner[:, None] == own_owner[None, :]
    earlier = lax.broadcasted_iota(jnp.int32, (requests, requests), 1) < lax.broadcasted_iota(
        jnp.int32, (requests, requests), 0
    )
    own_rank = jnp.sum(jnp.where(same_owner & earlier, 1, 0), axis=1).astype(jnp.int32)
    flat_slot = own_owner * slots + own_rank
    return (outgoing, flat_slot, slots)


def local(coords, skeleton, basis, probes, near_list, far_list):
    scale = 1.0 / math.sqrt(NEAR * LEAF)
    per_dev = near_list.shape[0]
    leaf_rows = per_dev * LEAF
    leaf_count = lax.axis_size("leaf")
    device_count = lax.axis_size(("oct", "leaf"))
    group_pos = lax.axis_index("oct")
    leaf_pos = lax.axis_index("leaf")
    dev_pos = lax.axis_index(("oct", "leaf"))
    first_leaf = dev_pos * per_dev
    group_first = group_pos * leaf_count * per_dev
    window_first = first_leaf - per_dev
    window = extended(probes, (("leaf", 0),), leaf_rows)
    window_leaf = window.reshape(3 * per_dev, LEAF, RHS)
    coords_leaf = coords.reshape(3, leaf_count * per_dev, LEAF)

    def near_leaf(local_pos):
        own_points = lax.dynamic_index_in_dim(
            coords_leaf, leaf_pos * per_dev + local_pos, 1, keepdims=False
        )
        near_ids = lax.dynamic_index_in_dim(near_list, local_pos, 0, keepdims=False)
        near_points = jnp.take(coords_leaf, near_ids - group_first, axis=1)
        dist_sq = jnp.square(own_points[0][None, :, None] - near_points[0][:, None, :])
        dist_sq = dist_sq + jnp.square(own_points[1][None, :, None] - near_points[1][:, None, :])
        dist_sq = dist_sq + jnp.square(own_points[2][None, :, None] - near_points[2][:, None, :])
        panel = matern(dist_sq).astype(jnp.bfloat16)
        near_rows = jnp.take(window_leaf, near_ids - window_first, axis=0)
        return jnp.einsum("kij,kjh->ih", panel, near_rows, preferred_element_type=jnp.float32)

    near_sum = lax.map(near_leaf, jnp.arange(per_dev, dtype=jnp.int32))
    basis_leaf = basis.reshape(RANK, per_dev, LEAF)
    coef = jnp.einsum(
        "mal,alh->amh",
        basis_leaf,
        probes.reshape(per_dev, LEAF, RHS),
        preferred_element_type=jnp.float32,
    ).astype(jnp.bfloat16)
    own_far = lax.dynamic_slice_in_dim(far_list, first_leaf, per_dev, 0)
    far_flat = own_far.reshape(per_dev * FAR)
    outgoing, flat_slot, slots = outgoing_slots(
        coef, far_list, far_flat, per_dev, dev_pos, device_count, leaf_count
    )
    received = lax.all_to_all(outgoing, ("oct", "leaf"), split_axis=0, concat_axis=0, tiled=True)
    picked = jnp.take(received.reshape(device_count * slots, RANK, RHS), flat_slot, axis=0)
    own_skel = lax.dynamic_slice_in_dim(skeleton, first_leaf, per_dev, 2)
    far_skel = jnp.take(skeleton, far_flat, axis=2).reshape(3, RANK, per_dev, FAR)
    own_side = jnp.transpose(own_skel, (0, 2, 1))[:, :, None, :, None]
    far_side = jnp.transpose(far_skel, (0, 2, 3, 1))[:, :, :, None, :]
    skel_sq = jnp.square(own_side[0] - far_side[0])
    skel_sq = skel_sq + jnp.square(own_side[1] - far_side[1])
    skel_sq = skel_sq + jnp.square(own_side[2] - far_side[2])
    coupling = matern(skel_sq).astype(jnp.bfloat16)
    picked_leaf = picked.reshape(per_dev, FAR, RANK, RHS)
    far_coef = jnp.einsum(
        "akmn,aknh->amh", coupling, picked_leaf, preferred_element_type=jnp.float32
    ).astype(jnp.bfloat16)
    far_sum = jnp.einsum("mal,amh->alh", basis_leaf, far_coef, preferred_element_type=jnp.float32)
    combined = ((near_sum + far_sum) * scale).astype(jnp.bfloat16)
    return combined.reshape(leaf_rows, RHS)


def solution(mesh):
    in_specs = (
        P(None, ("copies", "oct")),
        P(None, None, "copies"),
        P(None, ("copies", "oct", "leaf")),
        P(("copies", "oct", "leaf"), None),
        P(("copies", "oct", "leaf"), None),
        P("copies", None),
    )
    out_specs = P(("copies", "oct", "leaf"), None)
    return jax.shard_map(local, mesh=mesh, in_specs=in_specs, out_specs=out_specs, check_vma=False)
```

profile of v0, /device:TPU:1, one launch (start us, length us, event | category | flops | bytes accessed | tf_op | source)
XLA Modules:
  0.0 153.5 jit_solution(9647143809356026915)
XLA Ops:
  0.0 1.9 %collective-permute-start.1 = (bf16[2048,128]{1,0:T(8,128)(2,1)}, bf16[2048,128]{1,0:T(8,128)(2,1)S(1)}, u32[]{:S(2)}, u32[]{:S(2)}) collective-permute-start(bf16[2048,128]{1,0:T(8,128)(2,1)} %param.11), channel_id=1, source_target_pairs={{1,0},{2,1},{3,2},{5,4},{6,5},{7,6},{9,8},{10,9},{11,10},{13,12},{... | collective-permute-start | bytes 1572872 | tf_op jit(solution)/shard_map/ppermute | solution.py:27
  1.9 4.5 %collective-permute-start = (bf16[2048,128]{1,0:T(8,128)(2,1)}, bf16[2048,128]{1,0:T(8,128)(2,1)}, u32[]{:S(2)}, u32[]{:S(2)}) collective-permute-start(bf16[2048,128]{1,0:T(8,128)(2,1)} %param.11), channel_id=1, source_target_pairs={{0,1},{1,2},{2,3},{4,5},{5,6},{6,7},{8,9},{9,10},{10,11},{12,13},{... | collective-permute-start | bytes 1572872 | tf_op jit(solution)/shard_map/ppermute | solution.py:24
  6.4 0.7 add_select_fusion
  7.2 0.7 fusion.54
  8.1 0.1 fusion.49
  8.4 0.2 fusion.16
  8.6 0.1 copy.55
  8.7 1.3 convolution_convert_fusion.1
  10.0 0.6 convolution_convert_fusion
  10.7 1.5 copy.51
  12.2 5.4 %all-to-all-start = ((bf16[16,11,32,128]{3,2,1,0:T(8,128)(2,1)}), bf16[16,11,32,128]{3,2,1,0:T(8,128)(2,1)}, u32[]{:S(2)}, u32[]{:S(2)}) async-start(bf16[16,11,32,128]{3,2,1,0:T(8,128)(2,1)} %copy.51), calls=%async_computation | async-start | bytes 2883584 | tf_op jit(solution)/shard_map/all_to_all | solution.py:118
  17.9 0.2 select_reduce_fusion
  18.2 0.6 pad_clamp_fusion.2
  18.8 0.6 compare_and_fusion.2
  19.6 0.7 copy.45
  20.3 0.7 copy.44
  20.9 0.7 copy.41
  21.6 0.7 gather_fusion.2
  22.3 0.2 select_bitcast_fusion.1
  22.5 0.8 fusion.79
  23.4 0.8 copy-done.2
  24.2 1.3 pad_maximum_fusion
  25.6 121.5 %while.12 = (s32[]{:T(128)}, f32[4,512,128]{1,2,0:T(8,128)S(1)}, s32[4]{0:T(128)S(1)}, s32[]{:T(128)}, f32[3,16,512]{2,0,1:T(4,128)S(1)}, /*index=5*/s32[4,27]{1...) while((s32[]{:T(128)}, f32[4,512,128]{1,2,0:T(8,128)S(1)}, ...), condition=%wide.region_1.2_spmd, body=%wide.region_0.1_spmd.sunk | while | flops 1905765504 | bytes 12431286 | solution.py:105
  25.7 0.6 dynamic_slice.31
  28.3 0.7 compare_and_fusion.6
  29.0 2.8 %gather_fusion = bf16[27,512,128]{2,1,0:T(8,128)(2,1)} fusion(bf16[12,512,128]{2,1,0:T(8,128)(2,1)S(1)} %get-tuple-element.268, s32[1024]{0:T(1024)S(1)} %get-tuple-element.221), kind=kCustom, calls=%fused_computation.1.clone.1 | custom fusion | bytes 7077996 | tf_op jit(solution)/shard_map/while/body/eval_jaxpr/jit(_take)/gather | solution.py:102
  31.8 0.7 gather_fusion.1
  32.6 0.1 fusion.89
  33.5 22.5 %fusion.90 = f32[4,512,128]{1,2,0:T(8,128)S(1)} fusion(f32[4,512,128]{1,2,0:T(8,128)S(1)} %get-tuple-element.246, s32[]{:T(128)S(6)} %copy.93, bf16[27,512,128]{2,1,0:T(8,128)(2,1)} %gather_fusion, pred[27]{0:T(512)(128)(4,1)S(1)} %compare_and_fusion.7, f32[27,512]{1,0:T(8,128)S(1)} %bitcast.111, f32[512]{0:T(512)S(1)} %bitcast.123, ...), kind=kOutput, calls=%fused_computation.10.clone.1 | convolution fusion | flops 1905721344 | bytes 4004356 | tf_op jit(solution)/shard_map/while/body/eval_jaxpr/kij,kjh->ih/dot_general | solution.py:103
  56.0 0.6 dynamic_slice.31
  58.5 0.7 compare_and_fusion.6
  59.3 2.8 %gather_fusion = bf16[27,512,128]{2,1,0:T(8,128)(2,1)} fusion(bf16[12,512,128]{2,1,0:T(8,128)(2,1)S(1)} %get-tuple-element.268, s32[1024]{0:T(1024)S(1)} %get-tuple-element.221), kind=kCustom, calls=%fused_computation.1.clone.1 | custom fusion | bytes 7077996 | tf_op jit(solution)/shard_map/while/body/eval_jaxpr/jit(_take)/gather | solution.py:102
  62.1 0.7 gather_fusion.1
  63.7 22.5 %fusion.90 = f32[4,512,128]{1,2,0:T(8,128)S(1)} fusion(f32[4,512,128]{1,2,0:T(8,128)S(1)} %get-tuple-element.246, s32[]{:T(128)S(6)} %copy.93, bf16[27,512,128]{2,1,0:T(8,128)(2,1)} %gather_fusion, pred[27]{0:T(512)(128)(4,1)S(1)} %compare_and_fusion.7, f32[27,512]{1,0:T(8,128)S(1)} %bitcast.111, f32[512]{0:T(512)S(1)} %bitcast.123, ...), kind=kOutput, calls=%fused_computation.10.clone.1 | convolution fusion | flops 1905721344 | bytes 4004356 | tf_op jit(solution)/shard_map/while/body/eval_jaxpr/kij,kjh->ih/dot_general | solution.py:103
  86.3 0.6 dynamic_slice.31
  88.8 0.7 compare_and_fusion.6
  89.5 2.8 %gather_fusion = bf16[27,512,128]{2,1,0:T(8,128)(2,1)} fusion(bf16[12,512,128]{2,1,0:T(8,128)(2,1)S(1)} %get-tuple-element.268, s32[1024]{0:T(1024)S(1)} %get-tuple-element.221), kind=kCustom, calls=%fused_computation.1.clone.1 | custom fusion | bytes 7077996 | tf_op jit(solution)/shard_map/while/body/eval_jaxpr/jit(_take)/gather | solution.py:102
  92.4 0.7 gather_fusion.1
  94.0 22.5 %fusion.90 = f32[4,512,128]{1,2,0:T(8,128)S(1)} fusion(f32[4,512,128]{1,2,0:T(8,128)S(1)} %get-tuple-element.246, s32[]{:T(128)S(6)} %copy.93, bf16[27,512,128]{2,1,0:T(8,128)(2,1)} %gather_fusion, pred[27]{0:T(512)(128)(4,1)S(1)} %compare_and_fusion.7, f32[27,512]{1,0:T(8,128)S(1)} %bitcast.111, f32[512]{0:T(512)S(1)} %bitcast.123, ...), kind=kOutput, calls=%fused_computation.10.clone.1 | convolution fusion | flops 1905721344 | bytes 4004356 | tf_op jit(solution)/shard_map/while/body/eval_jaxpr/kij,kjh->ih/dot_general | solution.py:103
  116.6 0.6 dynamic_slice.31
  119.1 0.7 compare_and_fusion.6
  119.8 2.8 %gather_fusion = bf16[27,512,128]{2,1,0:T(8,128)(2,1)} fusion(bf16[12,512,128]{2,1,0:T(8,128)(2,1)S(1)} %get-tuple-element.268, s32[1024]{0:T(1024)S(1)} %get-tuple-element.221), kind=kCustom, calls=%fused_computation.1.clone.1 | custom fusion | bytes 7077996 | tf_op jit(solution)/shard_map/while/body/eval_jaxpr/jit(_take)/gather | solution.py:102
  122.6 0.7 gather_fusion.1
  124.3 22.5 %fusion.90 = f32[4,512,128]{1,2,0:T(8,128)S(1)} fusion(f32[4,512,128]{1,2,0:T(8,128)S(1)} %get-tuple-element.246, s32[]{:T(128)S(6)} %copy.93, bf16[27,512,128]{2,1,0:T(8,128)(2,1)} %gather_fusion, pred[27]{0:T(512)(128)(4,1)S(1)} %compare_and_fusion.7, f32[27,512]{1,0:T(8,128)S(1)} %bitcast.111, f32[512]{0:T(512)S(1)} %bitcast.123, ...), kind=kOutput, calls=%fused_computation.10.clone.1 | convolution fusion | flops 1905721344 | bytes 4004356 | tf_op jit(solution)/shard_map/while/body/eval_jaxpr/kij,kjh->ih/dot_general | solution.py:103
  147.0 2.2 %gather_fusion.3 = bf16[128,32,128]{2,1,0:T(8,128)(2,1)S(1)} fusion(bf16[176,32,128]{2,1,0:T(8,128)(2,1)} %bitcast.29, s32[1024]{0:T(1024)} %pad_clamp_fusion.2), kind=kCustom, calls=%fused_computation.3 | custom fusion | bytes 2097664 | tf_op jit(solution)/shard_map/jit(_take)/gather | solution.py:119
  149.4 2.9 %convolution_bitcast_fusion = f32[4,512,128]{1,2,0:T(8,128)S(1)} fusion(bf16[4,32,32,128]{3,2,1,0:T(8,128)(2,1)S(1)} %bitcast.114, f32[4,32,32]{2,1,0:T(8,128)S(1)} %bitcast.119, f32[4,32]{1,0:T(4,128)S(1)} %bitcast.124, f32[4,32,32]{2,1,0:T(8,128)} %bitcast.120, f32[4,32]{1,0:T(4,128)S(1)} %bitcast.125, f32[4,32,32]{2,1,0:T(8,128)S(1)} %bitcast.118, ...), kind=kOutput, calls=%fused_computation.35 | convolution fusion | flops 52576256 | bytes 2279040 | tf_op jit(solution)/shard_map/mal,amh->alh/dot_general | solution.py:132
  152.3 0.3 multiply_convert_fusion.9
  152.5 1.0 copy.54
  (78 shorter events, 2.1 us)
Async XLA Ops:
  0.0 23.4 %collective-permute-start.1 = (bf16[2048,128]{1,0:T(8,128)(2,1)}, bf16[2048,128]{1,0:T(8,128)(2,1)S(1)}, u32[]{:S(2)}, u32[]{:S(2)}) collective-permute-start(bf16[2048,128]{1,0:T(8,128)(2,1)} %param.11), channel_id=1, source_target_pairs={{1,0},{2,1},{3,2},{5,4},{6,5},{7,6},{9,8},{10,9},{11,10},{13,12},{... | collective-permute-start | bytes 1572872 | tf_op jit(solution)/shard_map/ppermute | solution.py:27
  1.9 22.2 %collective-permute-start = (bf16[2048,128]{1,0:T(8,128)(2,1)}, bf16[2048,128]{1,0:T(8,128)(2,1)}, u32[]{:S(2)}, u32[]{:S(2)}) collective-permute-start(bf16[2048,128]{1,0:T(8,128)(2,1)} %param.11), channel_id=1, source_target_pairs={{0,1},{1,2},{2,3},{4,5},{5,6},{6,7},{8,9},{9,10},{10,11},{12,13},{... | collective-permute-start | bytes 1572872 | tf_op jit(solution)/shard_map/ppermute | solution.py:24
  10.6 7.0 %copy-start.4 = (s32[64,32]{0,1:T(8,128)S(1)}, s32[64,32]{0,1:T(8,128)}, u32[]{:S(2)}) copy-start(s32[64,32]{0,1:T(8,128)} %param.13) | copy-start | bytes 24580
  10.7 8.7 %copy-start.3 = (f32[3,32,64]{2,1,0:T(8,128)S(1)}, f32[3,32,64]{2,1,0:T(8,128)}, u32[]{:S(2)}) copy-start(f32[3,32,64]{2,1,0:T(8,128)} %param.9) | copy-start | bytes 73732
  10.7 13.5 %copy-start.1 = (bf16[2048,128]{1,0:T(8,128)(2,1)S(1)}, bf16[2048,128]{1,0:T(8,128)(2,1)}, u32[]{:S(2)}) copy-start(bf16[2048,128]{1,0:T(8,128)(2,1)} %param.11) | copy-start | bytes 1572868
  12.2 13.3 %copy-start = (f32[3,8192]{1,0:T(4,128)S(1)}, f32[3,8192]{1,0:T(4,128)}, u32[]{:S(2)}) copy-start(f32[3,8192]{1,0:T(4,128)} %param.8) | copy-start | bytes 294916
  12.2 134.8 %all-to-all-start = ((bf16[16,11,32,128]{3,2,1,0:T(8,128)(2,1)}), bf16[16,11,32,128]{3,2,1,0:T(8,128)(2,1)}, u32[]{:S(2)}, u32[]{:S(2)}) async-start(bf16[16,11,32,128]{3,2,1,0:T(8,128)(2,1)} %copy.51), calls=%async_computation | async-start | bytes 2883584 | tf_op jit(solution)/shard_map/all_to_all | solution.py:118
  23.4 0.8 copy-start.2
  25.5 123.8 %copy-start.5 = (bf16[32,2048]{1,0:T(8,128)(2,1)S(1)}, bf16[32,2048]{1,0:T(8,128)(2,1)}, u32[]{:S(2)}) copy-start(bf16[32,2048]{1,0:T(8,128)(2,1)} %param.10) | copy-start | bytes 393220
  25.5 123.8 %copy-start.6 = (f32[1,4,32,32]{3,0,2,1:T(1,128)S(1)}, f32[1,4,32,32]{3,0,2,1:T(1,128)}, u32[]{:S(2)}) copy-start(f32[1,4,32,32]{3,0,2,1:T(1,128)} %get-tuple-element.141) | copy-start | bytes 49156
  25.5 123.8 %copy-start.7 = (f32[1,4,32,32]{3,0,2,1:T(1,128)S(1)}, f32[1,4,32,32]{3,0,2,1:T(1,128)}, u32[]{:S(2)}) copy-start(f32[1,4,32,32]{3,0,2,1:T(1,128)} %get-tuple-element.142) | copy-start | bytes 49156
  25.5 123.8 %copy-start.8 = (f32[1,4,32]{2,1,0:T(4,128)S(1)}, f32[1,4,32]{2,1,0:T(4,128)}, u32[]{:S(2)}) copy-start(f32[1,4,32]{2,1,0:T(4,128)} %copy.45) | copy-start | bytes 1540
  25.5 123.8 %copy-start.9 = (f32[1,4,32]{2,1,0:T(4,128)S(1)}, f32[1,4,32]{2,1,0:T(4,128)}, u32[]{:S(2)}) copy-start(f32[1,4,32]{2,1,0:T(4,128)} %copy.44) | copy-start | bytes 1540
  25.5 123.8 %copy-start.10 = (f32[1,4,32]{2,1,0:T(4,128)S(1)}, f32[1,4,32]{2,1,0:T(4,128)}, u32[]{:S(2)}) copy-start(f32[1,4,32]{2,1,0:T(4,128)} %copy.41) | copy-start | bytes 1540
  25.5 123.8 %copy-start.11 = (pred[4,32]{1,0:T(4,128)(4,1)S(1)}, pred[4,32]{1,0:T(4,128)(4,1)}, u32[]{:S(2)}) copy-start(pred[4,32]{1,0:T(4,128)(4,1)} %get-tuple-element.147) | copy-start | bytes 388
where the time goes:
time: 155 us; the launch traced here: 154 us
  matrix products  95.2 us (61%)
  local copies, waits for them, and re-layouts  27.2 us (18%)
  starting transfers between devices  11.8 us (8%)
  loops' own time  11.1 us (7%)
  other arithmetic  7.92 us (5%)
    dot_general x4, matrix products, near_leaf(): jnp.einsum('kij,kjh->ih', panel, near_rows, preferred_element_type=jnp.fl...  90.1 us
    gather x4, local copies, waits for them, and re-layouts, near_leaf(): near_rows = jnp.take(window_leaf, near_ids - window_first, axis=0)  11.3 us
    another operation x1, loops' own time, local(): near_sum = lax.map(near_leaf, jnp.arange(per_dev, dtype=jnp.int32))  11.1 us
    all_to_all x1, starting transfers between devices, local(): lax.all_to_all(outgoing, ('oct', 'leaf'), split_axis=0, concat_axis=0, ti...  5.38 us
    ppermute x1, starting transfers between devices, extended(): lax.ppermute(lax.slice_in_dim(block, block.shape[dim] - width, None, axis...  4.5 us
  transfers between devices with their start and end apart: 3, of which 0 were waited for; matrix products, arithmetic and copies ran while one was open for 80% of the time, Pallas kernels for 0%

commit v1 on v0

v1 whole, which is shorter than its diff:
```python
import functools
import math

import jax
import jax.numpy as jnp
from jax import lax
from jax.experimental import pallas as pl
from jax.experimental.pallas import tpu as pltpu
from jax.sharding import PartitionSpec as P

LEAF = 512
RANK = 32
RHS = 128
NEAR = 27
FAR = 32

LN2 = math.log(2.0)
UNIT = math.sqrt(3.0) / 0.4 / LN2
TINY = 1e-24
FEATURES = 64
MESH = pl.DeviceIdType.MESH
F32 = jnp.float32
BF16 = jnp.bfloat16


def split(x):
    first = x.astype(BF16).astype(F32)
    second = (x - first).astype(BF16).astype(F32)
    return first, second, x - first - second


def features(x, left):
    x1, x2, x3 = split(x)
    n1, n2, n3 = split(jnp.sum(x * x, axis=0, keepdims=True))
    row = lax.broadcasted_iota(jnp.int32, x.shape, 0)
    norm = jnp.where(row == 0, n1, jnp.where(row == 1, n2, jnp.where(row == 2, n3, 0.0)))
    ones = jnp.where(row < 3, 1.0, 0.0)
    if left:
        y1, y2, y3 = -2.0 * x1, -2.0 * x2, -2.0 * x3
        return jnp.concatenate([y1, y1, y2, y2, y1, y3, ones, norm], axis=0)
    return jnp.concatenate([x1, x2, x1, x2, x3, x1, norm, ones], axis=0)


def weighted(dist, weight):
    x = jnp.maximum(dist, TINY)
    s = x * lax.rsqrt(x)
    return ((weight + (weight * LN2) * s) * jnp.exp2(-s)).astype(BF16)


def kernel(
    n_oct, n_leaf, per_dev,
    coords_ref, skel_ref, basis_ref, probes_ref, near_ref, far_ref, out_ref,
    pts, skel, own_feat, acc, window, coefs, weights,
    near_send, near_recv, oct_send, oct_recv, leaf_send, leaf_recv,
):
    me_oct = lax.axis_index("oct")
    me = lax.axis_index("leaf")
    me_copy = lax.axis_index("copies")
    rows = per_dev * LEAF
    ranks = per_dev * RANK
    partner = me + 1 - 2 * lax.rem(me, 2)
    other = me - 1 + 2 * lax.rem(me, 2)
    sides = (partner, other)
    exists = [jnp.logical_and(side >= 0, side < n_leaf) for side in sides]

    def at(o, l):
        return (me_copy, o, l)

    barrier = pltpu.get_barrier_semaphore()
    for k in range(1, n_oct):
        pl.semaphore_signal(
            barrier, inc=1, device_id=at(lax.rem(me_oct + k, n_oct), me), device_id_type=MESH
        )
    for k in range(1, n_leaf):
        pl.semaphore_signal(
            barrier, inc=1, device_id=at(me_oct, lax.rem(me + k, n_leaf)), device_id_type=MESH
        )

    for j in range(per_dev):
        own = jnp.dot(
            basis_ref[:, j * LEAF:(j + 1) * LEAF],
            probes_ref[j * LEAF:(j + 1) * LEAF, :],
            preferred_element_type=F32,
        )
        coefs[me_oct, me, j * RANK:(j + 1) * RANK, :] = own.astype(BF16)

    pl.semaphore_wait(barrier, n_oct + n_leaf - 2)

    def near_copy(slot):
        return pltpu.make_async_remote_copy(
            src_ref=probes_ref, dst_ref=window.at[slot],
            send_sem=near_send.at[slot], recv_sem=near_recv.at[slot],
            device_id=at(me_oct, sides[slot]), device_id_type=MESH,
        )

    for slot in range(2):
        @pl.when(exists[slot])
        def _():
            near_copy(slot).start()

    pts[...] = jnp.zeros_like(pts)
    pts[0:3, :] = (coords_ref[...] - 0.5) * UNIT
    skel[...] = jnp.zeros_like(skel)
    skel[0:3, :] = (skel_ref[...] - 0.5) * UNIT
    own_x = pts[:, pl.ds(pl.multiple_of(me * rows, rows), rows)]
    own_feat[...] = features(own_x, False).astype(BF16)
    acc[...] = jnp.zeros_like(acc)
    near = near_ref[...]

    oct_copies = []
    for k in range(1, n_oct):
        oct_copies.append(pltpu.make_async_remote_copy(
            src_ref=coefs.at[me_oct, me], dst_ref=coefs.at[me_oct, me],
            send_sem=oct_send.at[k - 1], recv_sem=oct_recv.at[k - 1],
            device_id=at(lax.rem(me_oct + k, n_oct), me), device_id_type=MESH,
        ))
    for copy in oct_copies:
        copy.start()

    def near_block(source, read):
        first = (me_oct * n_leaf + source) * per_dev

        def body(c, carry):
            x = pts[:, pl.ds(pl.multiple_of(source * rows + c * LEAF, LEAF), LEAF)]
            left = features(x, True).T.astype(BF16)
            count = jnp.sum(
                jnp.where(near == first + c, 1.0, 0.0), axis=1, keepdims=True
            )
            weights[0:per_dev, :] = jnp.broadcast_to(count, (per_dev, LEAF))
            side = read(c).astype(F32).T.astype(BF16)
            for a in range(per_dev):
                cols = slice(a * LEAF, (a + 1) * LEAF)
                dist = jnp.dot(left, own_feat[:, cols], preferred_element_type=F32)
                panel = weighted(dist, weights[a:a + 1, :])
                acc[:, cols] += jnp.dot(side, panel, preferred_element_type=F32)
            return carry

        lax.fori_loop(0, per_dev, body, 0)

    near_block(me, lambda c: probes_ref[pl.ds(pl.multiple_of(c * LEAF, LEAF), LEAF), :])

    for copy in oct_copies:
        copy.wait()
    leaf_copies = []
    for k in range(1, n_leaf):
        leaf_copies.append(pltpu.make_async_remote_copy(
            src_ref=coefs.at[:, me], dst_ref=coefs.at[:, me],
            send_sem=leaf_send.at[k - 1], recv_sem=leaf_recv.at[k - 1],
            device_id=at(me_oct, lax.rem(me + k, n_leaf)), device_id_type=MESH,
        ))
    for copy in leaf_copies:
        copy.start()

    for slot in range(2):
        @pl.when(exists[slot])
        def _():
            near_copy(slot).wait()
            near_block(
                sides[slot],
                lambda c: window[slot, pl.ds(pl.multiple_of(c * LEAF, LEAF), LEAF), :],
            )

    for copy in leaf_copies:
        copy.wait()

    dev = me_oct * n_leaf + me
    mine = skel[:, pl.ds(pl.multiple_of(dev * ranks, ranks), ranks)]
    left = features(mine, True).T.astype(BF16)
    far = far_ref[...]
    far_coef = jnp.zeros((ranks, RHS), F32)
    for o in range(n_oct):
        width = n_leaf * ranks
        right = features(skel[:, o * width:(o + 1) * width], False).astype(BF16)
        dist = jnp.dot(left, right, preferred_element_type=F32)
        leaf_id = lax.broadcasted_iota(jnp.int32, (per_dev, width), 1) // RANK + o * n_leaf * per_dev
        count = jnp.zeros((per_dev, width), F32)
        for j in range(FAR):
            count += jnp.where(far[:, j:j + 1] == leaf_id, 1.0, 0.0)
        weight = jnp.concatenate(
            [jnp.broadcast_to(count[a:a + 1, :], (RANK, width)) for a in range(per_dev)], axis=0
        )
        block = coefs[o].reshape(width, RHS)
        far_coef += jnp.dot(weighted(dist, weight), block, preferred_element_type=F32)
    far_side = far_coef.T.astype(BF16)
    scale = 1.0 / math.sqrt(NEAR * LEAF)
    owner = lax.broadcasted_iota(jnp.int32, (ranks, LEAF), 0) // RANK
    for a in range(per_dev):
        cols = slice(a * LEAF, (a + 1) * LEAF)
        tiled = jnp.concatenate([basis_ref[:, cols].astype(F32)] * per_dev, axis=0)
        block = jnp.where(owner == a, tiled, 0.0).astype(BF16)
        total = acc[:, cols] + jnp.dot(far_side, block, preferred_element_type=F32)
        out_ref[cols, :] = (total * scale).T.astype(BF16)


def local(coords, skeleton, basis, probes, near_list, far_list):
    per_dev = near_list.shape[0]
    n_leaf = lax.axis_size("leaf")
    n_oct = lax.axis_size("oct")
    rows = per_dev * LEAF
    ranks = per_dev * RANK
    leaves = n_oct * n_leaf * per_dev
    dev = lax.axis_index(("oct", "leaf"))
    own_far = lax.dynamic_slice_in_dim(far_list, dev * per_dev, per_dev, 0)
    skel = jnp.transpose(skeleton, (0, 2, 1)).reshape(3, leaves * RANK)
    vmem = pl.BlockSpec(memory_space=pltpu.VMEM)
    return pl.pallas_call(
        functools.partial(kernel, n_oct, n_leaf, per_dev),
        out_shape=jax.ShapeDtypeStruct((rows, RHS), BF16),
        in_specs=[vmem] * 6,
        out_specs=vmem,
        scratch_shapes=[
            pltpu.VMEM((8, n_leaf * rows), F32),
            pltpu.VMEM((8, leaves * RANK), F32),
            pltpu.VMEM((FEATURES, rows), BF16),
            pltpu.VMEM((RHS, rows), F32),
            pltpu.VMEM((2, rows, RHS), BF16),
            pltpu.VMEM((n_oct, n_leaf, ranks, RHS), BF16),
            pltpu.VMEM((8, LEAF), F32),
            pltpu.SemaphoreType.DMA((2,)),
            pltpu.SemaphoreType.DMA((2,)),
            pltpu.SemaphoreType.DMA((n_oct - 1,)),
            pltpu.SemaphoreType.DMA((n_oct - 1,)),
            pltpu.SemaphoreType.DMA((n_leaf - 1,)),
            pltpu.SemaphoreType.DMA((n_leaf - 1,)),
        ],
        compiler_params=pltpu.CompilerParams(
            collective_id=0, has_side_effects=True, vmem_limit_bytes=60 * 1024 * 1024
        ),
    )(coords, skel, basis, probes, near_list, own_far)


def solution(mesh):
    in_specs = (
        P(None, ("copies", "oct")),
        P(None, None, "copies"),
        P(None, ("copies", "oct", "leaf")),
        P(("copies", "oct", "leaf"), None),
        P(("copies", "oct", "leaf"), None),
        P("copies", None),
    )
    out_specs = P(("copies", "oct", "leaf"), None)
    return jax.shard_map(local, mesh=mesh, in_specs=in_specs, out_specs=out_specs, check_vma=False)
```

time: 155 us -> 40.1 us (0.26)
  matrix products: 95.2 us -> 0 us
  Pallas kernels: 0 us -> 35.7 us
  local copies, waits for them, and re-layouts: 27.2 us -> 4.14 us
  starting transfers between devices: 11.8 us -> 0 us
  loops' own time: 11.1 us -> 0 us
  other arithmetic: 7.92 us -> 0 us
    dot_general x9 -> x0, matrix products: 95.2 us -> none  [the longest x4 90.1 us: near_leaf(): jnp.einsum('kij,kjh->ih', panel, near_rows, preferred_element_type=jnp.fl...]
    pallas_call x0 -> x1, Pallas kernels: none -> 35.7 us  [local(): pl.pallas_call(functools.partial(kernel, n_oct, n_leaf, per_dev), out_sha...]
    gather x10 -> x0, local copies, waits for them, and re-layouts: 17 us -> none  [the longest x4 11.3 us: near_leaf(): near_rows = jnp.take(window_leaf, near_ids - window_first, axis=0)]
    another operation x1 -> x0, loops' own time: 11.1 us -> none  [local(): near_sum = lax.map(near_leaf, jnp.arange(per_dev, dtype=jnp.int32))]
    ppermute x2 -> x0, starting transfers between devices: 6.41 us -> none  [the longest x1 4.5 us: extended(): lax.ppermute(lax.slice_in_dim(block, block.shape[dim] - width, None, axis...]
    all_to_all x1 -> x0, starting transfers between devices: 5.38 us -> none  [local(): lax.all_to_all(outgoing, ('oct', 'leaf'), split_axis=0, concat_axis=0, ti...]
    and x9 -> x0, other arithmetic: 3.38 us -> none  [the longest x4 2.79 us: near_leaf(): near_points = jnp.take(coords_leaf, near_ids - group_first, axis=1)]
    slice x13 -> x0, local copies, waits for them, and re-layouts: 3.3 us -> none  [the longest x3 1.48 us: local(): skel_sq = jnp.square(own_side[0] - far_side[0])]
  transfers between devices with their start and end apart: 3 -> 0, of which waited for: 0 -> 0; matrix products, arithmetic and copies ran while one was open for 80% -> 0% of each run, Pallas kernels for 0% -> 0%
where the time goes in v1:
time: 40.1 us; the launch traced here: 39.9 us
  Pallas kernels  35.7 us (89%)
  local copies, waits for them, and re-layouts  4.14 us (10%)
    pallas_call x1, Pallas kernels, local(): pl.pallas_call(functools.partial(kernel, n_oct, n_leaf, per_dev), out_sha...  35.7 us
    unnamed x6, local copies, waits for them, and re-layouts  3.24 us

profile of v1, /device:TPU:1, one launch (start us, length us, event | category | flops | bytes accessed | tf_op | source)
XLA Modules:
  0.0 39.9 jit_solution(12871953022462373536)
XLA Ops:
  0.0 0.0 copy-start
  0.0 0.0 copy-start.1
  0.0 0.7 %copy-done = s32[64,32]{0,1:T(8,128)S(1)} copy-done((s32[64,32]{0,1:T(8,128)S(1)}, s32[64,32]{0,1:T(8,128)}, u32[]{:S(2)}) %copy-start) | copy-done | bytes 8216
  0.7 0.1 constant_dynamic-slice_fusion
  0.8 0.7 %copy.11.far_ref = s32[4,32]{1,0:T(4,128)} copy(s32[4,32]{0,1:T(8,128)S(1)} %constant_dynamic-slice_fusion) | data formatting | bytes 1024
  1.4 0.0 copy-done.1
  1.5 0.1 copy.9
  1.5 0.7 %reshape.3.skel_ref = f32[3,2048]{1,0:T(4,128)} reshape(f32[3,64,32]{2,1,0:T(8,128)S(1)} %copy.9) | data formatting | bytes 49152 | tf_op jit(solution)/shard_map/reshape | solution.py:204
  2.3 35.7 %shard_map.64 = bf16[2048,128]{1,0:T(8,128)(2,1)} custom-call(f32[3,8192]{1,0:T(4,128)} %coords_ref.1, f32[3,2048]{1,0:T(4,128)} %reshape.3.skel_ref, bf16[32,2048]{1,0:T(8,128)(2,1)} %basis_ref.1, bf16[2048,128]{1,0:T(8,128)(2,1)} %probes_ref.1, s32[4,27]{1,0:T(4,128)} %near_ref.1, s32[4,32]{1,0:T(4,128)} %copy.11.far_ref), custom_call_target="tpu_custom_call" | custom-call | tf_op jit(solution)/shard_map/pallas_call | solution.py:206
  38.0 1.9 %copy.13 = bf16[2048,128]{1,0:T(8,128)(2,1)} copy(bf16[2048,128]{1,0:T(8,128)(2,1)} %shard_map.64) | data formatting | bytes 1048576
Async XLA Ops:
  0.0 0.7 %copy-start = (s32[64,32]{0,1:T(8,128)S(1)}, s32[64,32]{0,1:T(8,128)}, u32[]{:S(2)}) copy-start(s32[64,32]{0,1:T(8,128)} %param.11) | copy-start | bytes 24580
  0.0 1.4 %copy-start.1 = (f32[3,32,64]{2,1,0:T(8,128)S(1)}, f32[3,32,64]{2,1,0:T(8,128)}, u32[]{:S(2)}) copy-start(f32[3,32,64]{2,1,0:T(8,128)} %param.7) | copy-start | bytes 73732

commit v2 on v1

--- a/solution.py
+++ b/solution.py
@@ -15,7 +15,7 @@
 FAR = 32
 
 LN2 = math.log(2.0)
-UNIT = math.sqrt(3.0) / 0.4 / LN2
+UNIT = math.sqrt(3.0) / 0.4
 TINY = 1e-24
 FEATURES = 64
 MESH = pl.DeviceIdType.MESH
@@ -41,16 +41,17 @@
     return jnp.concatenate([x1, x2, x1, x2, x3, x1, norm, ones], axis=0)
 
 
-def weighted(dist, weight):
+def matern(dist):
     x = jnp.maximum(dist, TINY)
-    s = x * lax.rsqrt(x)
-    return ((weight + (weight * LN2) * s) * jnp.exp2(-s)).astype(BF16)
+    t = x * lax.rsqrt(x)
+    return (1.0 + t) * jnp.exp2(t * (-1.0 / LN2))
 
 
 def kernel(
     n_oct, n_leaf, per_dev,
     coords_ref, skel_ref, basis_ref, probes_ref, near_ref, far_ref, out_ref,
     pts, skel, own_feat, acc, window, coefs, weights,
+    dist_even, dist_odd, panel_even, panel_odd, side_even, side_odd, left_even, left_odd,
     near_send, near_recv, oct_send, oct_recv, leaf_send, leaf_recv,
 ):
     me_oct = lax.axis_index("oct")
@@ -88,15 +89,16 @@
 
     def near_copy(slot):
         return pltpu.make_async_remote_copy(
-            src_ref=probes_ref, dst_ref=window.at[slot],
+            src_ref=probes_ref, dst_ref=window.at[slot + 1],
             send_sem=near_send.at[slot], recv_sem=near_recv.at[slot],
             device_id=at(me_oct, sides[slot]), device_id_type=MESH,
         )
 
-    for slot in range(2):
-        @pl.when(exists[slot])
-        def _():
-            near_copy(slot).start()
+    near_copy(0).start()
+
+    @pl.when(exists[1])
+    def _():
+        near_copy(1).start()
 
     pts[...] = jnp.zeros_like(pts)
     pts[0:3, :] = (coords_ref[...] - 0.5) * UNIT
@@ -117,30 +119,6 @@
     for copy in oct_copies:
         copy.start()
 
-    def near_block(source, read):
-        first = (me_oct * n_leaf + source) * per_dev
-
-        def body(c, carry):
-            x = pts[:, pl.ds(pl.multiple_of(source * rows + c * LEAF, LEAF), LEAF)]
-            left = features(x, True).T.astype(BF16)
-            count = jnp.sum(
-                jnp.where(near == first + c, 1.0, 0.0), axis=1, keepdims=True
-            )
-            weights[0:per_dev, :] = jnp.broadcast_to(count, (per_dev, LEAF))
-            side = read(c).astype(F32).T.astype(BF16)
-            for a in range(per_dev):
-                cols = slice(a * LEAF, (a + 1) * LEAF)
-                dist = jnp.dot(left, own_feat[:, cols], preferred_element_type=F32)
-                panel = weighted(dist, weights[a:a + 1, :])
-                acc[:, cols] += jnp.dot(side, panel, preferred_element_type=F32)
-            return carry
-
-        lax.fori_loop(0, per_dev, body, 0)
-
-    near_block(me, lambda c: probes_ref[pl.ds(pl.multiple_of(c * LEAF, LEAF), LEAF), :])
-
-    for copy in oct_copies:
-        copy.wait()
     leaf_copies = []
     for k in range(1, n_leaf):
         leaf_copies.append(pltpu.make_async_remote_copy(
@@ -148,17 +126,96 @@
             send_sem=leaf_send.at[k - 1], recv_sem=leaf_recv.at[k - 1],
             device_id=at(me_oct, lax.rem(me + k, n_leaf)), device_id_type=MESH,
         ))
-    for copy in leaf_copies:
-        copy.start()
-
-    for slot in range(2):
-        @pl.when(exists[slot])
+
+    dists, panels = (dist_even, dist_odd), (panel_even, panel_odd)
+    lefts, side_refs = (left_even, left_odd), (side_even, side_odd)
+    total = (2 + exists[1].astype(jnp.int32)) * per_dev
+
+    def source_of(g):
+        slot = g // per_dev
+        return jnp.where(slot == 0, me, jnp.where(slot == 1, partner, other))
+
+    def fill_left(g, ref):
+        g = jnp.minimum(g, total - 1)
+        start = source_of(g) * rows + lax.rem(g, per_dev) * LEAF
+        ref[...] = features(pts[:, pl.ds(pl.multiple_of(start, LEAF), LEAF)], True).T.astype(BF16)
+
+    def fill_side(g, ref):
+        start = pl.multiple_of(lax.rem(g, per_dev) * LEAF, LEAF)
+        ref[...] = window[g // per_dev, pl.ds(start, LEAF), :].astype(F32).T.astype(BF16)
+
+    def fill_dist(half, ref, left, a):
+        part = slice(half * LEAF // 2, (half + 1) * LEAF // 2)
+        ref[part, :] = jnp.dot(
+            left[part, :], own_feat[:, a * LEAF:(a + 1) * LEAF], preferred_element_type=F32
+        )
+
+    def fill_panel(part, ref, dist):
+        for r in range(part * LEAF // 8, (part + 1) * LEAF // 8, 16):
+            ref[r:r + 16, :] = matern(dist[r:r + 16, :]).astype(BF16)
+
+    def apply(half, g, a, side, panel):
+        width = LEAF // 2
+        cols = slice(a * LEAF + half * width, a * LEAF + (half + 1) * width)
+        got = jnp.dot(
+            side[...], panel[:, half * width:(half + 1) * width], preferred_element_type=F32
+        )
+        acc[:, cols] += got * weights[g, a:a + 1, :width]
+
+    for g in range(3 * per_dev):
+        first = (me_oct * n_leaf + source_of(g)) * per_dev + g % per_dev
+        count = jnp.sum(jnp.where(near == first, 1.0, 0.0), axis=1, keepdims=True)
+        weights[g, 0:per_dev, :] = jnp.broadcast_to(count, (per_dev, LEAF // 2))
+    window[0] = probes_ref[...]
+    side_odd[...] = jnp.zeros_like(side_odd)
+    panel_odd[...] = jnp.zeros_like(panel_odd)
+    fill_left(0, left_even)
+    for half in range(2):
+        fill_dist(half, dist_even, left_even, 0)
+
+    steps = 2 * per_dev
+
+    def body(pair, carry):
+        g = pair * 2
+
+        @pl.when(g == per_dev)
         def _():
-            near_copy(slot).wait()
-            near_block(
-                sides[slot],
-                lambda c: window[slot, pl.ds(pl.multiple_of(c * LEAF, LEAF), LEAF), :],
-            )
+            near_copy(0).wait()
+            for copy in oct_copies:
+                copy.wait()
+            for copy in leaf_copies:
+                copy.start()
+
+        @pl.when(g == 2 * per_dev)
+        def _():
+            near_copy(1).wait()
+
+        for i in range(steps):
+            later = (i + 1) % steps
+            before = (i - 1) % steps
+            before_g = jnp.maximum(g - 1, 0) if i == 0 else g + before // per_dev
+            for part in range(8):
+                if part == 0 or part == 4:
+                    fill_dist(
+                        part // 4, dists[later % 2], lefts[later // per_dev], later % per_dev
+                    )
+                if part == 1 or part == 5:
+                    apply(
+                        part // 4, before_g, before % per_dev,
+                        side_refs[before // per_dev], panels[before % 2],
+                    )
+                if part == 6 and i == 0:
+                    fill_side(g, side_even)
+                    fill_left(g + 1, left_odd)
+                if part == 6 and i == per_dev:
+                    fill_side(g + 1, side_odd)
+                    fill_left(g + 2, left_even)
+                fill_panel(part, panels[i % 2], dists[i % 2])
+        return carry
+
+    lax.fori_loop(0, total // 2, body, 0)
+    for half in range(2):
+        apply(half, total - 1, per_dev - 1, side_odd, panel_odd)
 
     for copy in leaf_copies:
         copy.wait()
@@ -180,7 +237,7 @@
             [jnp.broadcast_to(count[a:a + 1, :], (RANK, width)) for a in range(per_dev)], axis=0
         )
         block = coefs[o].reshape(width, RHS)
-        far_coef += jnp.dot(weighted(dist, weight), block, preferred_element_type=F32)
+        far_coef += jnp.dot((matern(dist) * weight).astype(BF16), block, preferred_element_type=F32)
     far_side = far_coef.T.astype(BF16)
     scale = 1.0 / math.sqrt(NEAR * LEAF)
     owner = lax.broadcasted_iota(jnp.int32, (ranks, LEAF), 0) // RANK
@@ -213,9 +270,17 @@
             pltpu.VMEM((8, leaves * RANK), F32),
             pltpu.VMEM((FEATURES, rows), BF16),
             pltpu.VMEM((RHS, rows), F32),
-            pltpu.VMEM((2, rows, RHS), BF16),
+            pltpu.VMEM((3, rows, RHS), BF16),
             pltpu.VMEM((n_oct, n_leaf, ranks, RHS), BF16),
-            pltpu.VMEM((8, LEAF), F32),
+            pltpu.VMEM((3 * per_dev, 8, LEAF // 2), F32),
+            pltpu.VMEM((LEAF, LEAF), F32),
+            pltpu.VMEM((LEAF, LEAF), F32),
+            pltpu.VMEM((LEAF, LEAF), BF16),
+            pltpu.VMEM((LEAF, LEAF), BF16),
+            pltpu.VMEM((RHS, LEAF), BF16),
+            pltpu.VMEM((RHS, LEAF), BF16),
+            pltpu.VMEM((LEAF, FEATURES), BF16),
+            pltpu.VMEM((LEAF, FEATURES), BF16),
             pltpu.SemaphoreType.DMA((2,)),
             pltpu.SemaphoreType.DMA((2,)),
             pltpu.SemaphoreType.DMA((n_oct - 1,)),

time: 40.1 us -> 32.6 us (0.81)
  Pallas kernels: 35.7 us -> 28.2 us
    pallas_call x1, Pallas kernels: 35.7 us -> 28.2 us  [local(): pl.pallas_call(functools.partial(kernel, n_oct, n_leaf, per_dev), out_sha...]
where the time goes in v2:
time: 32.6 us; the launch traced here: 32.3 us
  Pallas kernels  28.2 us (87%)
  local copies, waits for them, and re-layouts  4.14 us (13%)
    pallas_call x1, Pallas kernels, local(): pl.pallas_call(functools.partial(kernel, n_oct, n_leaf, per_dev), out_sha...  28.2 us
    unnamed x6, local copies, waits for them, and re-layouts  3.24 us
    reshape x1, local copies, waits for them, and re-layouts, local(): skel = jnp.transpose(skeleton, (0, 2, 1)).reshape(3, leaves * RANK)  0.73 us

profile of v2, /device:TPU:1, one launch (start us, length us, event | category | flops | bytes accessed | tf_op | source)
XLA Modules:
  0.0 32.3 jit_solution(9039860265095024036)
XLA Ops:
  0.0 0.0 copy-start
  0.0 0.0 copy-start.1
  0.0 0.7 %copy-done = s32[64,32]{0,1:T(8,128)S(1)} copy-done((s32[64,32]{0,1:T(8,128)S(1)}, s32[64,32]{0,1:T(8,128)}, u32[]{:S(2)}) %copy-start) | copy-done | bytes 8216
  0.7 0.1 constant_dynamic-slice_fusion
  0.8 0.7 %copy.11.far_ref = s32[4,32]{1,0:T(4,128)} copy(s32[4,32]{0,1:T(8,128)S(1)} %constant_dynamic-slice_fusion) | data formatting | bytes 1024
  1.4 0.0 copy-done.1
  1.5 0.1 copy.9
  1.5 0.7 %reshape.3.skel_ref = f32[3,2048]{1,0:T(4,128)} reshape(f32[3,64,32]{2,1,0:T(8,128)S(1)} %copy.9) | data formatting | bytes 49152 | tf_op jit(solution)/shard_map/reshape | solution.py:261
  2.3 28.2 %shard_map.64 = bf16[2048,128]{1,0:T(8,128)(2,1)} custom-call(f32[3,8192]{1,0:T(4,128)} %coords_ref.1, f32[3,2048]{1,0:T(4,128)} %reshape.3.skel_ref, bf16[32,2048]{1,0:T(8,128)(2,1)} %basis_ref.1, bf16[2048,128]{1,0:T(8,128)(2,1)} %probes_ref.1, s32[4,27]{1,0:T(4,128)} %near_ref.1, s32[4,32]{1,0:T(4,128)} %copy.11.far_ref), custom_call_target="tpu_custom_call" | custom-call | tf_op jit(solution)/shard_map/pallas_call | solution.py:263
  30.5 1.9 %copy.13 = bf16[2048,128]{1,0:T(8,128)(2,1)} copy(bf16[2048,128]{1,0:T(8,128)(2,1)} %shard_map.64) | data formatting | bytes 1048576
Async XLA Ops:
  0.0 0.7 %copy-start = (s32[64,32]{0,1:T(8,128)S(1)}, s32[64,32]{0,1:T(8,128)}, u32[]{:S(2)}) copy-start(s32[64,32]{0,1:T(8,128)} %param.11) | copy-start | bytes 24580
  0.0 1.4 %copy-start.1 = (f32[3,32,64]{2,1,0:T(8,128)S(1)}, f32[3,32,64]{2,1,0:T(8,128)}, u32[]{:S(2)}) copy-start(f32[3,32,64]{2,1,0:T(8,128)} %param.7) | copy-start | bytes 73732

commit v3 on v2

--- a/solution.py
+++ b/solution.py
@@ -49,9 +49,10 @@
 
 def kernel(
     n_oct, n_leaf, per_dev,
-    coords_ref, skel_ref, basis_ref, probes_ref, near_ref, far_ref, out_ref,
+    coords_hbm, skel_hbm, basis_hbm, probes_hbm, near_hbm, far_hbm, out_ref,
     pts, skel, own_feat, acc, window, coefs, weights,
     dist_even, dist_odd, panel_even, panel_odd, side_even, side_odd, left_even, left_odd,
+    coords_ref, skel_ref, basis_ref, near_ref, far_ref, fetch_sem,
     near_send, near_recv, oct_send, oct_recv, leaf_send, leaf_recv,
 ):
     me_oct = lax.axis_index("oct")
@@ -67,6 +68,17 @@
     def at(o, l):
         return (me_copy, o, l)
 
+    probes_ref = window.at[0]
+    fetches = [
+        pltpu.make_async_copy(source, target, fetch_sem.at[n])
+        for n, (source, target) in enumerate((
+            (probes_hbm, probes_ref), (basis_hbm, basis_ref), (coords_hbm, coords_ref),
+            (near_hbm, near_ref), (skel_hbm, skel_ref), (far_hbm, far_ref),
+        ))
+    ]
+    for fetch in fetches:
+        fetch.start()
+
     barrier = pltpu.get_barrier_semaphore()
     for k in range(1, n_oct):
         pl.semaphore_signal(
@@ -77,6 +89,8 @@
             barrier, inc=1, device_id=at(me_oct, lax.rem(me + k, n_leaf)), device_id_type=MESH
         )
 
+    fetches[0].wait()
+    fetches[1].wait()
     for j in range(per_dev):
         own = jnp.dot(
             basis_ref[:, j * LEAF:(j + 1) * LEAF],
@@ -89,7 +103,7 @@
 
     def near_copy(slot):
         return pltpu.make_async_remote_copy(
-            src_ref=probes_ref, dst_ref=window.at[slot + 1],
+            src_ref=probes_hbm, dst_ref=window.at[slot + 1],
             send_sem=near_send.at[slot], recv_sem=near_recv.at[slot],
             device_id=at(me_oct, sides[slot]), device_id_type=MESH,
         )
@@ -100,6 +114,8 @@
     def _():
         near_copy(1).start()
 
+    for fetch in fetches[2:]:
+        fetch.wait()
     pts[...] = jnp.zeros_like(pts)
     pts[0:3, :] = (coords_ref[...] - 0.5) * UNIT
     skel[...] = jnp.zeros_like(skel)
@@ -166,7 +182,6 @@
         first = (me_oct * n_leaf + source_of(g)) * per_dev + g % per_dev
         count = jnp.sum(jnp.where(near == first, 1.0, 0.0), axis=1, keepdims=True)
         weights[g, 0:per_dev, :] = jnp.broadcast_to(count, (per_dev, LEAF // 2))
-    window[0] = probes_ref[...]
     side_odd[...] = jnp.zeros_like(side_odd)
     panel_odd[...] = jnp.zeros_like(panel_odd)
     fill_left(0, left_even)
@@ -223,7 +238,7 @@
     dev = me_oct * n_leaf + me
     mine = skel[:, pl.ds(pl.multiple_of(dev * ranks, ranks), ranks)]
     left = features(mine, True).T.astype(BF16)
-    far = far_ref[...]
+    far = far_ref[pl.ds(pl.multiple_of(dev * per_dev, per_dev), per_dev), :]
     far_coef = jnp.zeros((ranks, RHS), F32)
     for o in range(n_oct):
         width = n_leaf * ranks
@@ -256,14 +271,12 @@
     rows = per_dev * LEAF
     ranks = per_dev * RANK
     leaves = n_oct * n_leaf * per_dev
-    dev = lax.axis_index(("oct", "leaf"))
-    own_far = lax.dynamic_slice_in_dim(far_list, dev * per_dev, per_dev, 0)
     skel = jnp.transpose(skeleton, (0, 2, 1)).reshape(3, leaves * RANK)
     vmem = pl.BlockSpec(memory_space=pltpu.VMEM)
     return pl.pallas_call(
         functools.partial(kernel, n_oct, n_leaf, per_dev),
         out_shape=jax.ShapeDtypeStruct((rows, RHS), BF16),
-        in_specs=[vmem] * 6,
+        in_specs=[pl.BlockSpec(memory_space=pltpu.HBM)] * 6,
         out_specs=vmem,
         scratch_shapes=[
             pltpu.VMEM((8, n_leaf * rows), F32),
@@ -281,6 +294,12 @@
             pltpu.VMEM((RHS, LEAF), BF16),
             pltpu.VMEM((LEAF, FEATURES), BF16),
             pltpu.VMEM((LEAF, FEATURES), BF16),
+            pltpu.VMEM(coords.shape, F32),
+            pltpu.VMEM(skel.shape, F32),
+            pltpu.VMEM(basis.shape, BF16),
+            pltpu.VMEM(near_list.shape, jnp.int32),
+            pltpu.VMEM(far_list.shape, jnp.int32),
+            pltpu.SemaphoreType.DMA((6,)),
             pltpu.SemaphoreType.DMA((2,)),
             pltpu.SemaphoreType.DMA((2,)),
             pltpu.SemaphoreType.DMA((n_oct - 1,)),
@@ -291,7 +310,7 @@
         compiler_params=pltpu.CompilerParams(
             collective_id=0, has_side_effects=True, vmem_limit_bytes=60 * 1024 * 1024
         ),
-    )(coords, skel, basis, probes, near_list, own_far)
+    )(coords, skel, basis, probes, near_list, far_list)
 
 
 def solution(mesh):

time: 32.6 us -> 31.4 us (0.963)
  Pallas kernels: 28.2 us -> 27.1 us
    pallas_call x1, Pallas kernels: 28.2 us -> 27.1 us  [local(): pl.pallas_call(functools.partial(kernel, n_oct, n_leaf, per_dev), out_sha...]
    unnamed x6 -> x4, local copies, waits for them, and re-layouts: 3.24 us -> 3.29 us
where the time goes in v3:
time: 31.4 us; the launch traced here: 31.2 us
  Pallas kernels  27.1 us (86%)
  local copies, waits for them, and re-layouts  4.11 us (13%)
    pallas_call x1, Pallas kernels, local(): pl.pallas_call(functools.partial(kernel, n_oct, n_leaf, per_dev), out_sha...  27.1 us
    unnamed x4, local copies, waits for them, and re-layouts  3.29 us
    reshape x1, local copies, waits for them, and re-layouts, local(): skel = jnp.transpose(skeleton, (0, 2, 1)).reshape(3, leaves * RANK)  0.73 us

profile of v3, /device:TPU:1, one launch (start us, length us, event | category | flops | bytes accessed | tf_op | source)
XLA Modules:
  0.0 31.2 jit_solution(2711654132128392913)
XLA Ops:
  0.0 0.0 copy-start
  0.0 1.4 %copy.10.far_hbm = s32[64,32]{1,0:T(8,128)} copy(s32[64,32]{0,1:T(8,128)} %param.11) | data formatting | bytes 16384 | tf_op args[5]
  1.4 0.0 copy-done
  1.4 0.1 copy.9
  1.5 0.7 %reshape.3.skel_hbm = f32[3,2048]{1,0:T(4,128)} reshape(f32[3,64,32]{2,1,0:T(8,128)S(1)} %copy.9) | data formatting | bytes 49152 | tf_op jit(solution)/shard_map/reshape | solution.py:274
  2.2 27.1 %shard_map.64 = bf16[2048,128]{1,0:T(8,128)(2,1)} custom-call(f32[3,8192]{1,0:T(4,128)} %coords_hbm.1, f32[3,2048]{1,0:T(4,128)} %reshape.3.skel_hbm, bf16[32,2048]{1,0:T(8,128)(2,1)} %basis_hbm.1, bf16[2048,128]{1,0:T(8,128)(2,1)} %probes_hbm.1, s32[4,27]{1,0:T(4,128)} %near_hbm.1, s32[64,32]{1,0:T(8,128)} %copy.10.far_hbm), custom_call_target="tpu_custom_call" | custom-call | tf_op jit(solution)/shard_map/pallas_call | solution.py:276
  29.3 1.9 %copy.12 = bf16[2048,128]{1,0:T(8,128)(2,1)} copy(bf16[2048,128]{1,0:T(8,128)(2,1)} %shard_map.64) | data formatting | bytes 1048576
Async XLA Ops:
  0.0 1.4 %copy-start = (f32[3,32,64]{2,1,0:T(8,128)S(1)}, f32[3,32,64]{2,1,0:T(8,128)}, u32[]{:S(2)}) copy-start(f32[3,32,64]{2,1,0:T(8,128)} %param.7) | copy-start | bytes 73732
